TPU v7x, 32 devices: a whole 2x2x4 slice. The times are simulated.
32 devices in a mesh: elem: 8 (over z, core), lev: 4 (over y, x).
Axes of the slice: x: 2, y: 2, z: 4, core: 2. Of those that a mesh axis runs over, the one named last changes fastest.
Arguments:
- tracers: float32 [512, 16, 640], P('elem', 'lev'), may hold values from 0.1 to 120, as said below
- ref_index: int32 [512, 16], P('elem'), may hold values from 0 to 63
- requests: int32 [8, 2, 16], P('elem'), may hold values from -1 to 63, as said below
- source: int32 [512], P('elem'), may hold values from 0 to 95, as said below
- target_mean: float32 [40], replicated, may hold values from 0.5 to 5
Outputs:
- transported: float32 [512, 16, 640], P('elem', 'lev')
Inputs may be any that keep to these rules, and one draw needn't show every extreme that they name: Row 0 of requests[d] holds distinct element indices of block d - 1 (wrapping), row 1 of block d + 1; the valid entries come first and the rest are -1; every row holds 1 to 16 valid entries and some row holds exactly 16. `source`: every slot names an own element (below 64) or a valid entry of the block's requests: 64 + k for row 0, 80 + k for row 1. `tracers`: all entries are positive.
All inputs are finite; a program needn't handle non-finite values.
Results may differ from a plain program's by a relative error of at most 0.0003.
Values sent between devices are 32-bit elements; how exact they have to be, the bound alone decides.
A program may use at most 64 MiB of HBM per device.

v0:
```python
import math
import jax
import jax.numpy as jnp
from jax import lax
from jax.sharding import PartitionSpec as P

NPTS = 16
REFS = 64


def with_halo(cells, sides, width):
    for axis, dim in sides:
        count = lax.axis_size(axis)
        head = lax.slice_in_dim(cells, 0, width, axis=dim)
        tail = lax.slice_in_dim(cells, cells.shape[dim] - width, cells.shape[dim], axis=dim)
        cells = jnp.concatenate(
            [
                lax.ppermute(tail, axis, [(i, (i + 1) % count) for i in range(count)]),
                cells,
                lax.ppermute(head, axis, [((i + 1) % count, i) for i in range(count)]),
            ],
            axis=dim,
        )
    return cells


def lagrange_table():
    side = math.isqrt(REFS)
    gll_nodes = [-1.0, -math.sqrt(0.2), math.sqrt(0.2), 1.0]
    points = -1.0 + 2.0 * jnp.arange(side, dtype=jnp.float32) / (side - 1)
    columns = []
    for which in range(4):
        basis = jnp.ones((side,), jnp.float32)
        for other in range(4):
            if other != which:
                basis = basis * (points - gll_nodes[other]) / (gll_nodes[which] - gll_nodes[other])
        columns.append(basis)
    one_dim = jnp.stack(columns, axis=1)
    return (one_dim[:, None, :, None] * one_dim[None, :, None, :]).reshape(side * side, 16)


def quadrature():
    edge = jnp.array([1.0 / 6.0, 5.0 / 6.0, 5.0 / 6.0, 1.0 / 6.0], jnp.float32)
    return (edge[:, None] * edge[None, :]).reshape(16)


def interpolate(source_rows, ref_index):
    elem_count, levels, width = source_rows.shape
    onehot = (ref_index[:, :, None] == jnp.arange(REFS, dtype=jnp.int32)[None, None, :]).astype(
        jnp.float32
    )
    matrix = jnp.einsum("epr,rn->epn", onehot, lagrange_table(), precision=lax.Precision.HIGHEST)
    values = source_rows.reshape(elem_count, levels * (width // 16), 16)
    result = jnp.einsum("epn,ecn->ecp", matrix, values, precision=lax.Precision.HIGHEST)
    lowest = jnp.min(values, axis=2, keepdims=True)
    highest = jnp.max(values, axis=2, keepdims=True)
    result = jnp.minimum(jnp.maximum(result, lowest), highest)
    return result.reshape(elem_count, levels, width)


def per_device(tracers, ref_index, requests, source, target_mean):
    elem_count, levels, width = tracers.shape
    beside_all = with_halo(tracers, (("elem", 0),), elem_count)
    own_pos = jnp.arange(elem_count, 2 * elem_count, dtype=jnp.int32)
    left_pos = jnp.maximum(requests[0, 0], 0)
    right_pos = 2 * elem_count + jnp.maximum(requests[0, 1], 0)
    slot_pos = jnp.concatenate([own_pos, left_pos, right_pos])
    source_rows = beside_all[slot_pos[source]]
    clipped = interpolate(source_rows, ref_index)
    tracer_count = width // NPTS
    shaped = clipped.reshape(elem_count, levels, tracer_count, NPTS)
    local_mass = jnp.einsum("eltn,n->t", shaped, quadrature(), precision=lax.Precision.HIGHEST)
    column_mass = lax.psum(local_mass, "lev")
    global_mass = lax.psum(column_mass, "elem")
    whole_weight = 4.0 * elem_count * lax.axis_size("elem") * levels * lax.axis_size("lev")
    factor = target_mean * whole_weight / global_mass
    return (shaped * factor[None, None, :, None]).reshape(elem_count, levels, width)


def solution(mesh):
    placed = (P("elem", "lev", None), P("elem", None), P("elem", None, None), P("elem"), P())
    return jax.shard_map(
        per_device, mesh=mesh, in_specs=placed, out_specs=P("elem", "lev", None), check_vma=False
    )
```

profile of v0, /device:TPU:0, one launch (start us, length us, event | category | flops | bytes accessed | tf_op | source)
XLA Modules:
  0.0 54.3 jit_solution(1006085163537011619)
XLA Ops:
  0.0 4.5 %collective-permute-start.1 = (f32[64,4,640]{2,1,0:T(4,128)}, f32[64,4,640]{2,1,0:T(4,128)S(1)}, u32[]{:S(2)}, u32[]{:S(2)}) collective-permute-start(f32[64,4,640]{2,1,0:T(4,128)} %param.6), channel_id=1, source_target_pairs={{4,0},{8,4},{12,8},{16,12},{20,16},{24,20},{28,24},{0,28},{5,1},{9... | collective-permute-start | bytes 1966088 | tf_op jit(solution)/shard_map/ppermute | solution.py:20
  4.6 0.8 %maximum_bitcast_fusion = (s32[16]{0:T(128)S(1)}, s32[16]{0:T(128)S(1)}) fusion(s32[1,2,16]{2,1,0:T(2,128)} %param.8), kind=kLoop, calls=%fused_computation.29 | loop fusion | flops 48 | bytes 256 | tf_op jit(solution)/shard_map/max | solution.py:65
  5.4 0.1 reshape.146
  5.5 1.5 %fusion.1 = f32[64,16,16]{0,2,1:T(8,128)S(1)} fusion(f32[64,16,1]{0,1,2:T(8,128)S(1)} %reshape.146, s32[64,16]{0,1:T(8,128)} %param.7), kind=kOutput, calls=%fused_computation.8 | convolution fusion | flops 12648448 | bytes 73728 | tf_op jit(solution)/shard_map/epr,rn->epn/dot_general | solution.py:52
  7.0 1.0 %copy.23 = f32[64,16,16]{2,1,0:T(8,128)} copy(f32[64,16,16]{0,2,1:T(8,128)S(1)} %fusion.1) | data formatting | bytes 131072 | tf_op jit(solution)/shard_map/epr,rn->epn/dot_general | solution.py:52
  8.0 0.8 %broadcast_multiply_fusion.1 = f32[4,4]{1,0:T(4,128)S(1)} fusion(f32[4]{0:T(128)} %constant.76.clone), kind=kLoop, calls=%fused_computation.16 | loop fusion | flops 16 | bytes 80 | tf_op jit(solution)/shard_map/mul | solution.py:44
  8.8 0.1 reshape.147
  9.0 0.7 %compare_select_fusion.1 = s32[64]{0:T(128)S(1)} fusion(s32[64]{0:T(128)} %param.9), kind=kLoop, calls=%fused_computation.14 | loop fusion | flops 192 | bytes 512 | tf_op jit(solution)/shard_map/select_n | solution.py:68
  9.6 0.8 %gather_fusion = s32[64]{0:T(128)S(1)} fusion(s32[96]{0:T(128)S(1)} %pad_add_fusion, s32[1024]{0:T(1024)S(1)} %pad_clamp_fusion.1), kind=kCustom, calls=%fused_computation | custom fusion | bytes 768 | tf_op jit(solution)/shard_map/gather | solution.py:68
  10.4 7.6 %collective-permute-done.1 = f32[64,4,640]{2,1,0:T(4,128)S(1)} collective-permute-done((f32[64,4,640]{2,1,0:T(4,128)}, f32[64,4,640]{2,1,0:T(4,128)S(1)}, u32[]{:S(2)}, u32[]{:S(2)}) %collective-permute-start.1) | collective-permute-done | bytes 655392 | tf_op jit(solution)/shard_map/ppermute | solution.py:20
  18.0 3.0 %collective-permute-done = f32[64,4,640]{2,1,0:T(4,128)} collective-permute-done((f32[64,4,640]{2,1,0:T(4,128)}, f32[64,4,640]{2,1,0:T(4,128)}, u32[]{:S(2)}, u32[]{:S(2)}) %collective-permute-start) | collective-permute-done | bytes 655392 | tf_op jit(solution)/shard_map/ppermute | solution.py:18
  21.1 1.5 %pad_maximum_fusion = f32[192,4,640]{2,1,0:T(4,128)S(1)} fusion(f32[64,4,640]{2,1,0:T(4,128)S(1)} %collective-permute-done.1, f32[64,4,640]{2,1,0:T(4,128)S(1)} %copy-done, f32[64,4,640]{2,1,0:T(4,128)} %collective-permute-done), kind=kLoop, calls=%fused_computation.2 | loop fusion | flops 983040 | bytes 3932160 | tf_op jit(solution)/shard_map/concatenate | solution.py:16
  22.6 1.0 %gather_fusion.1 = f32[64,4,640]{2,1,0:T(4,128)S(1)} fusion(f32[192,4,640]{2,1,0:T(4,128)S(1)} %pad_maximum_fusion, s32[1024]{0:T(1024)S(1)} %pad_clamp_fusion), kind=kCustom, calls=%fused_computation.1 | custom fusion | bytes 1310976 | tf_op jit(solution)/shard_map/gather | solution.py:68
  23.5 0.4 copy.21
  24.0 0.5 fusion.7
  24.5 1.1 %copy.22 = f32[64,160,16]{1,2,0:T(8,128)S(1)} copy(f32[64,160,16]{0,2,1:T(8,128)S(1)} %bitcast.26) | data formatting | bytes 1310720 | tf_op jit(solution)/shard_map/reshape | solution.py:53
  25.8 2.1 %fusion.8 = (f32[160,16]{0,1:T(8,128)S(1)}, f32[64,160,16]{1,2,0:T(8,128)S(1)}) fusion(f32[64,160]{1,0:T(8,128)S(1)} %copy.25, f32[64,160]{1,0:T(8,128)S(1)} %copy.24, f32[64,160,16]{1,2,0:T(8,128)S(1)} %copy.22, f32[64,16,16]{2,1,0:T(8,128)} %copy.23), kind=kOutput, calls=%fused_computation.32 | convolution fusion | flops 31946240 | bytes 1468416 | tf_op jit(solution)/shard_map/epn,ecn->ecp/dot_general | solution.py:54
  28.0 0.1 reduce_sum.14
  28.1 0.1 convolution_bitcast_fusion
  28.2 9.9 %psum.14 = f32[40]{0:T(128)S(1)} all-reduce(f32[40]{0:T(128)S(1)} %convolution_bitcast_fusion), channel_id=1, replica_groups=mesh['elem'=8,'lev'=4] {'lev'}, use_global_device_ids=true, to_apply=%region_4.0 | all-reduce | flops 40 | bytes 320 | tf_op jit(solution)/shard_map/psum | solution.py:73
  38.1 13.6 %psum.15 = f32[40]{0:T(128)S(1)} all-reduce(f32[40]{0:T(128)S(1)} %psum.14), channel_id=1, replica_groups=mesh['elem'=8,'lev'=4] {'elem'}, use_global_device_ids=true, to_apply=%region_5.6 | all-reduce | flops 40 | bytes 320 | tf_op jit(solution)/shard_map/psum | solution.py:74
  51.8 1.1 %copy.26 = f32[64,160,16]{0,2,1:T(8,128)S(1)} copy(f32[64,160,16]{1,2,0:T(8,128)S(1)} %get-tuple-element.10) | data formatting | bytes 1310720 | tf_op jit(solution)/shard_map/min | solution.py:57
  52.9 0.2 bitcast_multiply_fusion
  53.1 1.2 %copy.27 = f32[64,4,640]{2,1,0:T(4,128)} copy(f32[64,4,640]{0,2,1:T(8,128)S(1)} %bitcast_multiply_fusion) | data formatting | bytes 1310720 | tf_op jit(solution)/shard_map/mul | solution.py:77
  (20 shorter events, 0.6 us)
Async XLA Ops:
  0.0 21.1 %copy-start = (f32[64,4,640]{2,1,0:T(4,128)S(1)}, f32[64,4,640]{2,1,0:T(4,128)}, u32[]{:S(2)}) copy-start(f32[64,4,640]{2,1,0:T(4,128)} %param.6) | copy-start | bytes 1966084
  0.0 18.0 %collective-permute-start.1 = (f32[64,4,640]{2,1,0:T(4,128)}, f32[64,4,640]{2,1,0:T(4,128)S(1)}, u32[]{:S(2)}, u32[]{:S(2)}) collective-permute-start(f32[64,4,640]{2,1,0:T(4,128)} %param.6), channel_id=1, source_target_pairs={{4,0},{8,4},{12,8},{16,12},{20,16},{24,20},{28,24},{0,28},{5,1},{9... | collective-permute-start | bytes 1966088 | tf_op jit(solution)/shard_map/ppermute | solution.py:20
  4.5 16.5 %collective-permute-start = (f32[64,4,640]{2,1,0:T(4,128)}, f32[64,4,640]{2,1,0:T(4,128)}, u32[]{:S(2)}, u32[]{:S(2)}) collective-permute-start(f32[64,4,640]{2,1,0:T(4,128)} %param.6), channel_id=1, source_target_pairs={{0,4},{4,8},{8,12},{12,16},{16,20},{20,24},{24,28},{28,0},{1,5},{5... | collective-permute-start | bytes 1966088 | tf_op jit(solution)/shard_map/ppermute | solution.py:18
  25.6 26.1 %copy-start.1 = (f32[40]{0:T(128)S(1)}, f32[40]{0:T(128)}, u32[]{:S(2)}) copy-start(f32[40]{0:T(128)} %param.10) | copy-start | bytes 484
where the time goes:
time: 54.6 us; the launch traced here: 54.3 us
  blocking collectives  23.5 us (43%)
  waiting for transfers between devices  10.6 us (19%)
  local copies, waits for them, and re-layouts  7.18 us (13%)
  other arithmetic  4.66 us (9%)
  starting transfers between devices  4.52 us (8%)
  matrix products  3.75 us (7%)
    psum x1, blocking collectives, per_device(): global_mass = lax.psum(column_mass, 'elem')  13.6 us
    psum x1, blocking collectives, per_device(): column_mass = lax.psum(local_mass, 'lev')  9.89 us
    ppermute x1, waiting for transfers between devices, with_halo(): lax.ppermute(head, axis, [((i + 1) % count, i) for i in range(count)])  7.59 us
    ppermute x1, starting transfers between devices, with_halo(): lax.ppermute(head, axis, [((i + 1) % count, i) for i in range(count)])  4.52 us
    ppermute x1, waiting for transfers between devices, with_halo(): lax.ppermute(tail, axis, [(i, (i + 1) % count) for i in range(count)])  3.03 us
    gather x3, local copies, waits for them, and re-layouts, per_device(): source_rows = beside_all[slot_pos[source]]  2.17 us
    dot_general x1, matrix products, interpolate(): jnp.einsum('epn,ecn->ecp', matrix, values, precision=lax.Precision.HIGHEST)  2.15 us
    concatenate x1, other arithmetic, with_halo(): jnp.concatenate([lax.ppermute(tail, axis, [(i, (i + 1) % count) for i in...  1.51 us
  transfers between devices with their start and end apart: 2, of which 2 were waited for; matrix products, arithmetic and copies ran while one was open for 11% of the time, Pallas kernels for 0%

commit v1 on v0

--- a/solution.py
+++ b/solution.py
@@ -71,7 +71,7 @@
     shaped = clipped.reshape(elem_count, levels, tracer_count, NPTS)
     local_mass = jnp.einsum("eltn,n->t", shaped, quadrature(), precision=lax.Precision.HIGHEST)
     column_mass = lax.psum(local_mass, "lev")
-    global_mass = lax.psum(column_mass, "elem")
+    global_mass = jnp.sum(lax.all_gather(column_mass, "elem"), axis=0)
     whole_weight = 4.0 * elem_count * lax.axis_size("elem") * levels * lax.axis_size("lev")
     factor = target_mean * whole_weight / global_mass
     return (shaped * factor[None, None, :, None]).reshape(elem_count, levels, width)

time: 54.6 us -> 50.8 us (0.930)
  blocking collectives: 23.5 us -> 19.7 us
    psum x1 -> x0, blocking collectives: 13.6 us -> none  [per_device(): global_mass = lax.psum(column_mass, 'elem')]
    all_gather x0 -> x1, blocking collectives: none -> 9.8 us  [per_device(): global_mass = jnp.sum(lax.all_gather(column_mass, 'elem'), axis=0)]
  transfers between devices with their start and end apart: 2 -> 2, of which waited for: 2 -> 2; matrix products, arithmetic and copies ran while one was open for 11% -> 12% of each run, Pallas kernels for 0% -> 0%
where the time goes in v1:
time: 50.8 us; the launch traced here: 50.6 us
  blocking collectives  19.7 us (39%)
  waiting for transfers between devices  10.6 us (21%)
  local copies, waits for them, and re-layouts  7.18 us (14%)
  other arithmetic  4.69 us (9%)
  starting transfers between devices  4.52 us (9%)
  matrix products  3.75 us (7%)
    psum x1, blocking collectives, per_device(): column_mass = lax.psum(local_mass, 'lev')  9.89 us
    all_gather x1, blocking collectives, per_device(): global_mass = jnp.sum(lax.all_gather(column_mass, 'elem'), axis=0)  9.8 us
    ppermute x1, waiting for transfers between devices, with_halo(): lax.ppermute(head, axis, [((i + 1) % count, i) for i in range(count)])  7.59 us
    ppermute x1, starting transfers between devices, with_halo(): lax.ppermute(head, axis, [((i + 1) % count, i) for i in range(count)])  4.52 us
    ppermute x1, waiting for transfers between devices, with_halo(): lax.ppermute(tail, axis, [(i, (i + 1) % count) for i in range(count)])  3.03 us
    gather x3, local copies, waits for them, and re-layouts, per_device(): source_rows = beside_all[slot_pos[source]]  2.17 us
    dot_general x1, matrix products, interpolate(): jnp.einsum('epn,ecn->ecp', matrix, values, precision=lax.Precision.HIGHEST)  2.15 us
    concatenate x1, other arithmetic, with_halo(): jnp.concatenate([lax.ppermute(tail, axis, [(i, (i + 1) % count) for i in...  1.51 us
  transfers between devices with their start and end apart: 2, of which 2 were waited for; matrix products, arithmetic and copies ran while one was open for 12% of the time, Pallas kernels for 0%

profile of v1, /device:TPU:0, one launch (start us, length us, event | category | flops | bytes accessed | tf_op | source)
XLA Modules:
  0.0 50.6 jit_solution(4275211021458498185)
XLA Ops:
  0.0 4.5 %collective-permute-start.1 = (f32[64,4,640]{2,1,0:T(4,128)}, f32[64,4,640]{2,1,0:T(4,128)S(1)}, u32[]{:S(2)}, u32[]{:S(2)}) collective-permute-start(f32[64,4,640]{2,1,0:T(4,128)} %param.6), channel_id=1, source_target_pairs={{4,0},{8,4},{12,8},{16,12},{20,16},{24,20},{28,24},{0,28},{5,1},{9... | collective-permute-start | bytes 1966088 | tf_op jit(solution)/shard_map/ppermute | solution.py:20
  4.6 0.8 %maximum_bitcast_fusion = (s32[16]{0:T(128)S(1)}, s32[16]{0:T(128)S(1)}) fusion(s32[1,2,16]{2,1,0:T(2,128)} %param.8), kind=kLoop, calls=%fused_computation.28 | loop fusion | flops 48 | bytes 256 | tf_op jit(solution)/shard_map/max | solution.py:65
  5.4 0.1 reshape.148
  5.5 1.5 %fusion.1 = f32[64,16,16]{0,2,1:T(8,128)S(1)} fusion(f32[64,16,1]{0,1,2:T(8,128)S(1)} %reshape.148, s32[64,16]{0,1:T(8,128)} %param.7), kind=kOutput, calls=%fused_computation.7 | convolution fusion | flops 12648448 | bytes 73728 | tf_op jit(solution)/shard_map/epr,rn->epn/dot_general | solution.py:52
  7.0 1.0 %copy.23 = f32[64,16,16]{2,1,0:T(8,128)} copy(f32[64,16,16]{0,2,1:T(8,128)S(1)} %fusion.1) | data formatting | bytes 131072 | tf_op jit(solution)/shard_map/epr,rn->epn/dot_general | solution.py:52
  8.0 0.8 %broadcast_multiply_fusion.1 = f32[4,4]{1,0:T(4,128)S(1)} fusion(f32[4]{0:T(128)} %constant.76.clone), kind=kLoop, calls=%fused_computation.15 | loop fusion | flops 16 | bytes 80 | tf_op jit(solution)/shard_map/mul | solution.py:44
  8.8 0.1 reshape.149
  9.0 0.7 %compare_select_fusion.1 = s32[64]{0:T(128)S(1)} fusion(s32[64]{0:T(128)} %param.9), kind=kLoop, calls=%fused_computation.13 | loop fusion | flops 192 | bytes 512 | tf_op jit(solution)/shard_map/select_n | solution.py:68
  9.6 0.8 %gather_fusion = s32[64]{0:T(128)S(1)} fusion(s32[96]{0:T(128)S(1)} %pad_add_fusion, s32[1024]{0:T(1024)S(1)} %pad_clamp_fusion.1), kind=kCustom, calls=%fused_computation | custom fusion | bytes 768 | tf_op jit(solution)/shard_map/gather | solution.py:68
  10.4 7.6 %collective-permute-done.1 = f32[64,4,640]{2,1,0:T(4,128)S(1)} collective-permute-done((f32[64,4,640]{2,1,0:T(4,128)}, f32[64,4,640]{2,1,0:T(4,128)S(1)}, u32[]{:S(2)}, u32[]{:S(2)}) %collective-permute-start.1) | collective-permute-done | bytes 655392 | tf_op jit(solution)/shard_map/ppermute | solution.py:20
  18.0 3.0 %collective-permute-done = f32[64,4,640]{2,1,0:T(4,128)} collective-permute-done((f32[64,4,640]{2,1,0:T(4,128)}, f32[64,4,640]{2,1,0:T(4,128)}, u32[]{:S(2)}, u32[]{:S(2)}) %collective-permute-start) | collective-permute-done | bytes 655392 | tf_op jit(solution)/shard_map/ppermute | solution.py:18
  21.1 1.5 %pad_maximum_fusion = f32[192,4,640]{2,1,0:T(4,128)S(1)} fusion(f32[64,4,640]{2,1,0:T(4,128)S(1)} %collective-permute-done.1, f32[64,4,640]{2,1,0:T(4,128)S(1)} %copy-done, f32[64,4,640]{2,1,0:T(4,128)} %collective-permute-done), kind=kLoop, calls=%fused_computation.2 | loop fusion | flops 983040 | bytes 3932160 | tf_op jit(solution)/shard_map/concatenate | solution.py:16
  22.6 1.0 %gather_fusion.1 = f32[64,4,640]{2,1,0:T(4,128)S(1)} fusion(f32[192,4,640]{2,1,0:T(4,128)S(1)} %pad_maximum_fusion, s32[1024]{0:T(1024)S(1)} %pad_clamp_fusion), kind=kCustom, calls=%fused_computation.1 | custom fusion | bytes 1310976 | tf_op jit(solution)/shard_map/gather | solution.py:68
  23.5 0.4 copy.21
  24.0 0.5 %fusion.7 = (f32[64,160]{0,1:T(8,128)S(1)}, f32[64,160]{0,1:T(8,128)S(1)}) fusion(f32[64,160,16]{0,2,1:T(8,128)S(1)} %bitcast.25), kind=kLoop, calls=%fused_computation.30 | loop fusion | flops 307200 | bytes 737280 | tf_op jit(solution)/shard_map/reduce_min | solution.py:55
  24.5 1.1 %copy.22 = f32[64,160,16]{1,2,0:T(8,128)S(1)} copy(f32[64,160,16]{0,2,1:T(8,128)S(1)} %bitcast.26) | data formatting | bytes 1310720 | tf_op jit(solution)/shard_map/reshape | solution.py:53
  25.8 2.1 %fusion.8 = (f32[160,16]{0,1:T(8,128)S(1)}, f32[64,160,16]{1,2,0:T(8,128)S(1)}) fusion(f32[64,160]{1,0:T(8,128)S(1)} %copy.25, f32[64,160]{1,0:T(8,128)S(1)} %copy.24, f32[64,160,16]{1,2,0:T(8,128)S(1)} %copy.22, f32[64,16,16]{2,1,0:T(8,128)} %copy.23), kind=kOutput, calls=%fused_computation.31 | convolution fusion | flops 31946240 | bytes 1468416 | tf_op jit(solution)/shard_map/epn,ecn->ecp/dot_general | solution.py:54
  28.0 0.1 reduce_sum.26
  28.1 0.1 fusion.9
  28.2 9.9 %psum.7 = f32[1,40]{1,0:T(1,128)S(1)} all-reduce(f32[1,40]{1,0:T(1,128)S(1)} %fusion.9), channel_id=1, replica_groups=mesh['elem'=8,'lev'=4] {'lev'}, use_global_device_ids=true, to_apply=%region_4.0 | all-reduce | flops 40 | bytes 320 | tf_op jit(solution)/shard_map/psum | solution.py:73
  38.1 9.8 %all-gather = f32[8,1,40]{2,1,0:T(1,128)S(1)} all-gather(f32[1,1,40]{2,1,0:T(1,128)S(1)} %bitcast.28), channel_id=1, replica_groups=mesh['elem'=8,'lev'=4] {'elem'}, dimensions={0}, use_global_device_ids=true | all-gather | bytes 1440 | tf_op jit(solution)/shard_map/all_gather | solution.py:74
  48.1 1.1 %copy.26 = f32[64,160,16]{0,2,1:T(8,128)S(1)} copy(f32[64,160,16]{1,2,0:T(8,128)S(1)} %get-tuple-element.10) | data formatting | bytes 1310720 | tf_op jit(solution)/shard_map/min | solution.py:57
  49.2 0.2 bitcast_multiply_fusion
  49.3 1.2 %copy.27 = f32[64,4,640]{2,1,0:T(4,128)} copy(f32[64,4,640]{0,2,1:T(8,128)S(1)} %bitcast_multiply_fusion) | data formatting | bytes 1310720 | tf_op jit(solution)/shard_map/mul | solution.py:77
  (21 shorter events, 0.6 us)
Async XLA Ops:
  0.0 21.1 %copy-start = (f32[64,4,640]{2,1,0:T(4,128)S(1)}, f32[64,4,640]{2,1,0:T(4,128)}, u32[]{:S(2)}) copy-start(f32[64,4,640]{2,1,0:T(4,128)} %param.6) | copy-start | bytes 1966084
  0.0 18.0 %collective-permute-start.1 = (f32[64,4,640]{2,1,0:T(4,128)}, f32[64,4,640]{2,1,0:T(4,128)S(1)}, u32[]{:S(2)}, u32[]{:S(2)}) collective-permute-start(f32[64,4,640]{2,1,0:T(4,128)} %param.6), channel_id=1, source_target_pairs={{4,0},{8,4},{12,8},{16,12},{20,16},{24,20},{28,24},{0,28},{5,1},{9... | collective-permute-start | bytes 1966088 | tf_op jit(solution)/shard_map/ppermute | solution.py:20
  4.5 16.5 %collective-permute-start = (f32[64,4,640]{2,1,0:T(4,128)}, f32[64,4,640]{2,1,0:T(4,128)}, u32[]{:S(2)}, u32[]{:S(2)}) collective-permute-start(f32[64,4,640]{2,1,0:T(4,128)} %param.6), channel_id=1, source_target_pairs={{0,4},{4,8},{8,12},{12,16},{16,20},{20,24},{24,28},{28,0},{1,5},{5... | collective-permute-start | bytes 1966088 | tf_op jit(solution)/shard_map/ppermute | solution.py:18
  25.6 22.3 %copy-start.1 = (f32[40]{0:T(128)S(1)}, f32[40]{0:T(128)}, u32[]{:S(2)}) copy-start(f32[40]{0:T(128)} %param.10) | copy-start | bytes 484
